TPU v7x, 32 devices: a whole 2x2x4 slice. The times are simulated.
32 devices in a mesh: band: 8 (over z, y), dir: 4 (over x, core).
Axes of the slice: x: 2, y: 2, z: 4, core: 2. Of those that a mesh axis runs over, the one named last changes fastest.
Arguments:
- visibilities: float32 [8, 2, 2, 2, 16, 512], P('band'), may hold values from -6 to 6
- coherencies: float32 [8, 16, 2, 2, 2, 16, 512], P('band', 'dir'), may hold values from -1.2 to 1.2
- jones_start: float32 [8, 16, 2, 2, 2, 1024], P('band', 'dir'), may hold values from -3.6 to 3.6
- dual_start: float32 [8, 16, 2, 2, 2, 1024], P('band', 'dir'), may hold values from -6 to 6
- consensus_start: float32 [8, 16, 2, 2, 2, 1024], P(None, 'dir'), may hold values from -1.8 to 1.8
- freq_basis: float32 [8, 8], P('band'), may hold values from -1 to 1
- baseline_station_pairs: int32 [2, 512], replicated, may hold values from 0 to 1023
Outputs:
- jones_final: float32 [8, 16, 2, 2, 2, 1024], P('band', 'dir')
- dual_final: float32 [8, 16, 2, 2, 2, 1024], P('band', 'dir')
- consensus_coeffs: float32 [8, 16, 2, 2, 2, 1024], P(None, 'dir')
All inputs are finite; a program needn't handle non-finite values.
Results may differ from a plain program's by a relative error of at most 0.0003.
Values sent between devices are 32-bit elements; how exact they have to be, the bound alone decides.
A program may use at most 128 MiB of HBM per device.

v0:
```python
import jax
import jax.numpy as jnp
from jax import lax
from jax.sharding import PartitionSpec as P

ITERS = 3


RHO = 5.0
RIDGE = 0.25


def small_mul(left, right):
    return left[:, 0:1] * right[0:1] + left[:, 1:2] * right[1:2]


def complex_mul(left, right):
    real_part = small_mul(left[0], right[0]) - small_mul(left[1], right[1])
    imag_part = small_mul(left[0], right[1]) + small_mul(left[1], right[0])
    return jnp.stack([real_part, imag_part])


def hermitian(value):
    return jnp.stack([jnp.swapaxes(value[0], 0, 1), -jnp.swapaxes(value[1], 0, 1)])


def solve_right(numer, matrix):
    adjugate = jnp.stack(
        [
            jnp.stack([matrix[:, 1, 1], -matrix[:, 0, 1]], axis=1),
            jnp.stack([-matrix[:, 1, 0], matrix[:, 0, 0]], axis=1),
        ],
        axis=1,
    )
    det_real = (
        matrix[0, 0, 0] * matrix[0, 1, 1]
        - matrix[1, 0, 0] * matrix[1, 1, 1]
        - (matrix[0, 0, 1] * matrix[0, 1, 0] - matrix[1, 0, 1] * matrix[1, 1, 0])
    )
    det_imag = (
        matrix[0, 0, 0] * matrix[1, 1, 1]
        + matrix[1, 0, 0] * matrix[0, 1, 1]
        - (matrix[0, 0, 1] * matrix[1, 1, 0] + matrix[1, 0, 1] * matrix[0, 1, 0])
    )
    product = complex_mul(numer, adjugate)
    divisor = det_real * det_real + det_imag * det_imag
    real_part = (product[0] * det_real + product[1] * det_imag) / divisor
    imag_part = (product[1] * det_real - product[0] * det_imag) / divisor
    return jnp.stack([real_part, imag_part])


def predict(jones_k, coher_k, first, second):
    jones_first = jnp.take(jones_k, first, axis=-1)[..., None, :]
    jones_second = jnp.take(jones_k, second, axis=-1)[..., None, :]
    return complex_mul(complex_mul(jones_first, coher_k), hermitian(jones_second))


def baseline_terms(target, jones_k, coher_k, first, second):
    jones_first = jnp.take(jones_k, first, axis=-1)[..., None, :]
    jones_second = jnp.take(jones_k, second, axis=-1)[..., None, :]
    along_term = complex_mul(coher_k, hermitian(jones_second))
    back_term = hermitian(complex_mul(jones_first, coher_k))
    flipped = hermitian(target)
    right_first = jnp.sum(complex_mul(target, hermitian(along_term)), axis=-2)
    normal_first = jnp.sum(complex_mul(along_term, hermitian(along_term)), axis=-2)
    right_second = jnp.sum(complex_mul(flipped, hermitian(back_term)), axis=-2)
    normal_second = jnp.sum(complex_mul(back_term, hermitian(back_term)), axis=-2)
    first_part = jnp.concatenate([right_first.reshape(8, -1), normal_first.reshape(8, -1)], axis=0)
    second_part = jnp.concatenate(
        [right_second.reshape(8, -1), normal_second.reshape(8, -1)], axis=0
    )
    return jnp.concatenate([first_part, second_part], axis=1)


def update_one(right_sum, normal_sum, consensus, dual):
    identity = jnp.stack([jnp.eye(2, dtype=jnp.float32), jnp.zeros((2, 2), jnp.float32)])[..., None]
    matrix = normal_sum + RHO * identity
    return solve_right(right_sum + RHO * consensus - dual, matrix)


def apply_inverse(scale_factor, sums):
    flat = sums.reshape(sums.shape[0], -1)
    return jax.scipy.linalg.cho_solve((scale_factor, True), flat).reshape(sums.shape)


def local(
    visibilities,
    coherencies,
    jones_start,
    dual_start,
    consensus_start,
    freq_basis,
    baseline_station_pairs,
):
    coefficient_row = freq_basis[0]
    terms = coefficient_row.shape[0]
    outer = coefficient_row[:, None] * coefficient_row[None, :]
    gram = lax.psum(outer, "band") + RIDGE * lax.axis_size("band") * jnp.eye(
        terms, dtype=jnp.float32
    )
    scale_factor = jnp.linalg.cholesky(gram)
    first = baseline_station_pairs[0]
    second = baseline_station_pairs[1]
    stations = jones_start.shape[-1]
    station_ids = jnp.arange(stations, dtype=jnp.int32)
    onehots = (jnp.concatenate([first, second])[:, None] == station_ids[None, :]).astype(
        jnp.float32
    )
    vis_band = visibilities[0]
    coher_band = coherencies[0]
    jones = jones_start[0]
    dual = dual_start[0]
    dirs = jones.shape[0]
    coeffs = consensus_start
    consensus = jnp.tensordot(coefficient_row, coeffs, axes=(0, 0), precision=lax.Precision.HIGHEST)
    for turn_index in range(ITERS):
        model_terms = jax.vmap(predict, (0, 0, None, None))(jones, coher_band, first, second)
        model_total = lax.psum(jnp.sum(model_terms, axis=0), "dir")
        residual = vis_band - model_total
        normal_terms = jax.vmap(baseline_terms, (0, 0, 0, None, None))(
            residual[None] + model_terms, jones, coher_band, first, second
        )
        stacked = normal_terms.reshape(dirs * 16, -1)
        segment = jnp.dot(stacked, onehots, precision=lax.Precision.HIGHEST)
        segment = segment.reshape((dirs, 2, 2, 2, 2, stations))
        jones = jax.vmap(update_one)(segment[:, 0], segment[:, 1], consensus, dual)
        local_terms = coefficient_row.reshape((terms, 1, 1, 1, 1, 1)) * (jones + dual / RHO)[None]
        coeff_sums = lax.psum(local_terms, "band")
        coeffs = apply_inverse(scale_factor, coeff_sums)
        consensus = jnp.tensordot(
            coefficient_row, coeffs, axes=(0, 0), precision=lax.Precision.HIGHEST
        )
        dual = dual + RHO * (jones - consensus)
    return (jones[None], dual[None], coeffs)


def solution(mesh):
    in_specs = (
        P("band", None, None, None, None, None),
        P("band", "dir", None, None, None, None, None),
        P("band", "dir", None, None, None, None),
        P("band", "dir", None, None, None, None),
        P(None, "dir", None, None, None, None),
        P("band", None),
        P(),
    )
    out_specs = (
        P("band", "dir", None, None, None, None),
        P("band", "dir", None, None, None, None),
        P(None, "dir", None, None, None, None),
    )
    return jax.shard_map(local, mesh=mesh, in_specs=in_specs, out_specs=out_specs, check_vma=False)
```

profile of v0, /device:TPU:0, one launch (start us, length us, event | category | flops | bytes accessed | tf_op | source)
XLA Modules:
  0.0 537.7 jit_solution(1846712404722757130)
XLA Ops:
  8.1 2.3 slice_bitcast_fusion.13
  10.4 4.4 copy.255
  14.8 7.1 %gather_fusion = f32[512,4,2,2,2]{1,4,3,2,0:T(2,128)} fusion(f32[4,2,2,2,1024]{0,3,4,2,1:T(2,128)} %bitcast.712, s32[1024]{0:T(1024)S(1)} %pad_clamp_fusion.1), kind=kCustom, calls=%fused_computation.clone | custom fusion | bytes 133120 | tf_op jit(solution)/shard_map/vmap(jit(_take))/gather | solution.py:53
  22.0 3.1 select_bitcast_fusion.5
  25.8 1.6 fusion.92
  28.2 7.2 %gather_fusion.1 = f32[512,4,2,2,2]{1,4,3,2,0:T(2,128)} fusion(f32[4,2,2,2,1024]{0,3,4,2,1:T(2,128)} %bitcast.713, s32[1024]{0:T(1024)S(1)} %pad_clamp_fusion), kind=kCustom, calls=%fused_computation.1.clone | custom fusion | bytes 133120 | tf_op jit(solution)/shard_map/vmap(jit(_take))/gather | solution.py:54
  35.4 3.4 select_bitcast_fusion.4
  39.6 2.6 fusion.90
  42.3 1.6 copy.267
  43.9 1.2 copy.265
  49.9 1.3 add_subtract_fusion.19
  51.4 1.3 slice_bitcast_fusion.100
  53.9 1.2 copy.269
  55.2 1.2 copy.268
  62.5 2.1 fusion.13
  64.8 23.1 %psum.51 = f32[8,8]{0,1:T(8,128)S(1)} all-reduce(f32[8,8]{0,1:T(8,128)S(1)} %broadcast_multiply_fusion.3), channel_id=1, replica_groups=mesh['band'=8,'dir'=4] {'band'}, use_global_device_ids=true, to_apply=%region_12.14 | all-reduce | flops 64 | bytes 512 | tf_op jit(solution)/shard_map/psum | solution.py:98
  92.5 1.3 fusion.19
  98.8 1.7 fusion.5
  101.2 4.6 copy.288
  105.8 7.1 %gather_fusion.2 = f32[512,4,2,2,2]{1,4,3,2,0:T(2,128)} fusion(f32[4,2,2,2,1024]{0,3,4,2,1:T(2,128)} %copy.288, s32[1024]{0:T(1024)S(1)} %pad_clamp_fusion.1), kind=kCustom, calls=%fused_computation.2.clone | custom fusion | bytes 133120 | tf_op jit(solution)/shard_map/vmap(jit(_take))/gather | solution.py:53
  112.9 7.1 %gather_fusion.3 = f32[512,4,2,2,2]{1,4,3,2,0:T(2,128)} fusion(f32[4,2,2,2,1024]{0,3,4,2,1:T(2,128)} %copy.288, s32[1024]{0:T(1024)S(1)} %copy-done.112), kind=kCustom, calls=%fused_computation.3.clone | custom fusion | bytes 133120 | tf_op jit(solution)/shard_map/vmap(jit(_take))/gather | solution.py:54
  120.1 3.0 select_bitcast_fusion.3
  123.8 1.8 fusion.89
  125.6 1.8 copy.292
  127.5 1.8 copy.291
  129.3 1.8 fusion.88
  131.1 1.8 copy.290
  132.9 1.8 copy.289
  139.2 1.3 add_subtract_fusion.10
  140.5 2.0 select_bitcast_fusion.2
  142.5 1.9 slice_bitcast_fusion.3
  148.4 2.5 fusion.86
  153.6 2.1 add_subtract_fusion.15
  155.7 1.2 add_subtract_fusion.13
  159.1 2.0 slice_bitcast_fusion.49
  161.1 1.9 slice_bitcast_fusion.51
  166.3 1.9 reshape.1424
  168.1 1.9 slice_bitcast_fusion.63
  170.6 18.1 %all-reduce.10.cloned.1.call-done = f32[2,2,2,16,512]{4,3,2,1,0:T(8,128)} async-done(((f32[2,2,2,16,512]{4,3,2,1,0:T(8,128)}), f32[2,2,2,16,512]{4,3,2,1,0:T(8,128)}) %all-reduce.10.cloned.1.call-update) | async-done | bytes 262160 | tf_op jit(solution)/shard_map/psum | solution.py:118
  189.7 1.3 fusion.17
  196.1 2.4 fusion.3
  198.6 72.6 %all-reduce.12.cloned.1.call-done = f32[8,32768]{1,0:T(8,128)} async-done(((f32[8,32768]{1,0:T(8,128)}), f32[8,32768]{1,0:T(8,128)}) %all-reduce.12.cloned.1.call-update) | async-done | bytes 1048592 | tf_op jit(solution)/shard_map/psum | solution.py:128
  271.1 2.3 fusion.68
  276.8 4.6 copy.327
  281.4 7.1 %gather_fusion.4 = f32[512,4,2,2,2]{1,4,3,2,0:T(2,128)} fusion(f32[4,2,2,2,1024]{0,3,4,2,1:T(2,128)} %copy.327, s32[1024]{0:T(1024)S(1)} %pad_clamp_fusion.1), kind=kCustom, calls=%fused_computation.4.clone | custom fusion | bytes 133120 | tf_op jit(solution)/shard_map/vmap(jit(_take))/gather | solution.py:53
  288.5 7.1 %gather_fusion.5 = f32[512,4,2,2,2]{1,4,3,2,0:T(2,128)} fusion(f32[4,2,2,2,1024]{0,3,4,2,1:T(2,128)} %copy.327, s32[1024]{0:T(1024)S(1)} %copy-done.113), kind=kCustom, calls=%fused_computation.5.clone | custom fusion | bytes 133120 | tf_op jit(solution)/shard_map/vmap(jit(_take))/gather | solution.py:54
  295.7 3.0 select_bitcast_fusion.1
  299.4 1.8 fusion.85
  302.4 1.2 copy.330
  303.7 1.8 fusion.84
  306.7 1.2 copy.328
  311.6 1.3 add_subtract_fusion.1
  312.9 2.0 select_bitcast_fusion
  315.0 1.9 slice_bitcast_fusion
  325.5 1.9 slice_bitcast_fusion.38
  329.8 1.9 reshape.1430
  333.0 22.8 %all-reduce.14.cloned.1.call-done = f32[2,2,2,16,512]{4,3,2,1,0:T(8,128)} async-done(((f32[2,2,2,16,512]{4,3,2,1,0:T(8,128)}), f32[2,2,2,16,512]{4,3,2,1,0:T(8,128)}) %all-reduce.14.cloned.1.call-update) | async-done | bytes 262160 | tf_op jit(solution)/shard_map/psum | solution.py:118
  361.9 1.7 fusion.1
  363.7 74.3 %all-reduce.16.cloned.1.call-done = f32[8,32768]{1,0:T(8,128)} async-done(((f32[8,32768]{1,0:T(8,128)}), f32[8,32768]{1,0:T(8,128)}) %all-reduce.16.cloned.1.call-update) | async-done | bytes 1048592 | tf_op jit(solution)/shard_map/psum | solution.py:128
  438.0 2.3 fusion.64
  443.6 1.9 reshape.1432
  446.3 77.2 %all-reduce.18.cloned.1.call-done = f32[8,32768]{1,0:T(8,128)} async-done(((f32[8,32768]{1,0:T(8,128)}), f32[8,32768]{1,0:T(8,128)}) %all-reduce.18.cloned.1.call-update) | async-done | bytes 1048592 | tf_op jit(solution)/shard_map/psum | solution.py:128
  523.5 2.3 fusion.60
  527.7 1.8 copy.368
  (468 shorter events, 83.9 us)
Async XLA Ops:
  7.2 55.4 %copy-start = (f32[8,4,2,2,2,1024]{5,4,3,2,1,0:T(2,128)S(1)}, f32[8,4,2,2,2,1024]{5,4,3,2,1,0:T(2,128)}, u32[]{:S(2)}) copy-start(f32[8,4,2,2,2,1024]{5,4,3,2,1,0:T(2,128)} %param.15) | copy-start | bytes 3145732
  7.2 3.2 copy-start.105
  7.2 84.3 %all-reduce.8.cloned.1.call-start = ((), (), s32[]{:S(2)}) async-start(), calls=%async_computation | async-start | bytes 524288 | tf_op jit(solution)/shard_map/psum | solution.py:118
  8.1 13.9 %copy-start.117 = (pred[512]{0:T(512)(128)(4,1)}, pred[512]{0:T(512)(128)(4,1)S(1)}, u32[]{:S(2)}) copy-start(pred[512]{0:T(512)(128)(4,1)S(1)} %compare_and_fusion) | copy-start | bytes 1540
  8.1 27.3 %copy-start.114 = (pred[512]{0:T(512)(128)(4,1)}, pred[512]{0:T(512)(128)(4,1)S(1)}, u32[]{:S(2)}) copy-start(pred[512]{0:T(512)(128)(4,1)S(1)} %compare_and_fusion.1) | copy-start | bytes 1540
  28.2 10.5 %copy-start.111 = (s32[1024]{0:T(1024)}, s32[1024]{0:T(1024)S(1)}, u32[]{:S(2)}) copy-start(s32[1024]{0:T(1024)S(1)} %pad_clamp_fusion) | copy-start | bytes 12292
  42.3 3.3 copy-start.8
  42.3 3.3 copy-start.9
  42.3 3.3 copy-start.6
  42.3 3.3 copy-start.7
  48.1 140.6 %all-reduce.10.cloned.1.call-start = ((), (), s32[]{:S(2)}) async-start(), calls=%async_computation.1 | async-start | bytes 524288 | tf_op jit(solution)/shard_map/psum | solution.py:118
  49.0 2.1 copy-start.10
  59.1 3.4 copy-start.110
  60.0 31.6 %copy-start.12 = (f32[1,2,2,2,16,512]{5,4,3,2,1,0:T(8,128)S(1)}, f32[1,2,2,2,16,512]{5,4,3,2,1,0:T(8,128)}, u32[]{:S(2)}) copy-start(f32[1,2,2,2,16,512]{5,4,3,2,1,0:T(8,128)} %param.11) | copy-start | bytes 786436
  101.1 4.7 copy-start.89
  101.2 4.7 copy-start.92
  101.2 11.7 %copy-start.112 = (s32[1024]{0:T(1024)S(1)}, s32[1024]{0:T(1024)}, u32[]{:S(2)}) copy-start(s32[1024]{0:T(1024)} %copy-done.111) | copy-start | bytes 12292
  101.2 18.9 %copy-start.118 = (pred[512]{0:T(512)(128)(4,1)S(1)}, pred[512]{0:T(512)(128)(4,1)}, u32[]{:S(2)}) copy-start(pred[512]{0:T(512)(128)(4,1)} %copy-done.117) | copy-start | bytes 1540
  135.7 3.5 copy-start.98
  135.8 3.5 copy-start.99
  135.8 3.5 copy-start.100
  135.8 3.5 copy-start.101
  137.5 3.0 copy-start.14
  137.5 3.0 copy-start.115
  152.5 3.2 copy-start.102
  152.5 3.2 copy-start.103
  152.5 3.2 copy-start.104
  153.5 3.4 copy-start.90
  153.5 3.4 copy-start.93
  153.5 4.2 copy-start.79
  153.5 4.2 copy-start.80
  153.5 4.2 copy-start.81
  153.6 4.2 copy-start.82
  153.6 4.2 copy-start.106
  153.6 4.2 copy-start.107
  153.6 4.2 copy-start.108
  153.6 4.2 copy-start.109
  158.1 5.8 %copy-start.4 = (f32[1,4,2,2,16,512]{5,4,3,2,1,0:T(8,128)}, f32[1,4,2,2,16,512]{5,4,3,2,1,0:T(8,128)S(1)}, u32[]{:S(2)}) copy-start(f32[1,4,2,2,16,512]{5,4,3,2,1,0:T(8,128)S(1)} %get-tuple-element.80) | copy-start | bytes 1572868
  158.1 5.8 %copy-start.5 = (f32[1,4,2,2,16,512]{5,4,3,2,1,0:T(8,128)}, f32[1,4,2,2,16,512]{5,4,3,2,1,0:T(8,128)S(1)}, u32[]{:S(2)}) copy-start(f32[1,4,2,2,16,512]{5,4,3,2,1,0:T(8,128)S(1)} %get-tuple-element.81) | copy-start | bytes 1572868
  159.0 112.1 %all-reduce.12.cloned.1.call-start = ((), (), s32[]{:S(2)}) async-start(), calls=%async_computation.2 | async-start | bytes 2097152 | tf_op jit(solution)/shard_map/psum | solution.py:128
  159.1 3.9 copy-start.22
  159.1 4.8 copy-start.21
  159.1 5.6 %copy-start.19 = (f32[4,2,2,16,512]{4,3,1,0,2:T(8,128)S(1)}, f32[4,2,2,16,512]{4,3,1,0,2:T(8,128)}, u32[]{:S(2)}) copy-start(f32[4,2,2,16,512]{4,3,1,0,2:T(8,128)} %get-tuple-element.79) | copy-start | bytes 1572868
  161.1 4.5 copy-start.95
  170.1 185.6 %all-reduce.14.cloned.1.call-start = ((), (), s32[]{:S(2)}) async-start(), calls=%async_computation.3 | async-start | bytes 524288 | tf_op jit(solution)/shard_map/psum | solution.py:118
  276.7 4.7 copy-start.83
  276.7 4.7 copy-start.86
  276.8 11.7 %copy-start.113 = (s32[1024]{0:T(1024)S(1)}, s32[1024]{0:T(1024)}, u32[]{:S(2)}) copy-start(s32[1024]{0:T(1024)} %copy-done.111) | copy-start | bytes 12292
  276.8 18.9 %copy-start.119 = (pred[512]{0:T(512)(128)(4,1)S(1)}, pred[512]{0:T(512)(128)(4,1)}, u32[]{:S(2)}) copy-start(pred[512]{0:T(512)(128)(4,1)} %copy-done.117) | copy-start | bytes 1540
  309.9 3.0 copy-start.13
  309.9 3.0 copy-start.116
  320.1 2.5 copy-start.75
  320.1 2.5 copy-start.76
  320.1 2.5 copy-start.77
  320.1 2.5 copy-start.78
  322.9 4.5 copy-start.20
  323.7 114.3 %all-reduce.16.cloned.1.call-start = ((), (), s32[]{:S(2)}) async-start(), calls=%async_computation.4 | async-start | bytes 2097152 | tf_op jit(solution)/shard_map/psum | solution.py:128
  323.7 4.5 copy-start.18
  324.6 4.5 copy-start.26
  324.6 4.5 copy-start.84
  324.6 4.5 copy-start.87
  329.1 2.6 copy-start.17
  332.7 190.8 %all-reduce.18.cloned.1.call-start = ((), (), s32[]{:S(2)}) async-start(), calls=%async_computation.5 | async-start | bytes 2097152 | tf_op jit(solution)/shard_map/psum | solution.py:128
  525.7 4.7 copy-start.1
  (65 other events, 82.5 us)
Sparse Core Ops, SparseCore 0:
  48.3 34.9 all-reduce.7
  159.1 29.5 all-reduce.9
  192.8 78.3 all-reduce.11
  323.8 31.8 all-reduce.13
  359.6 78.2 all-reduce.15
  445.6 77.8 all-reduce.17
where the time goes:
time: 548 us; the launch traced here: 538 us
  waiting for transfers between devices  265 us (48%)
  local copies, waits for them, and re-layouts  155 us (28%)
  other arithmetic  56.7 us (10%)
  blocking collectives  23.1 us (4%)
  matrix products  20.7 us (4%)
  between operations  16.6 us (3%)
    psum x3, waiting for transfers between devices, local(): coeff_sums = lax.psum(local_terms, 'band')  224 us
    mul x92, local copies, waits for them, and re-layouts, small_mul(): return left[:, 0:1] * right[0:1] + left[:, 1:2] * right[1:2]  57.9 us
    psum x3, waiting for transfers between devices, local(): model_total = lax.psum(jnp.sum(model_terms, axis=0), 'dir')  40.9 us
    psum x1, blocking collectives, local(): lax.psum(outer, 'band')  23.1 us
    gather x3, local copies, waits for them, and re-layouts, predict(): jones_second = jnp.take(jones_k, second, axis=-1)[..., None, :]  21.4 us
    gather x3, local copies, waits for them, and re-layouts, predict(): jones_first = jnp.take(jones_k, first, axis=-1)[..., None, :]  21.3 us
    slice x10, local copies, waits for them, and re-layouts, small_mul(): return left[:, 0:1] * right[0:1] + left[:, 1:2] * right[1:2]  16.4 us
    unnamed x250, local copies, waits for them, and re-layouts  15.9 us
  transfers between devices with their start and end apart: 6, of which 5 were waited for; matrix products, arithmetic and copies ran while one was open for 10% of the time, Pallas kernels for 0%

commit v1 on v0

v1 whole, which is shorter than its diff:
```python
import functools

import jax
import jax.numpy as jnp
from jax import lax
from jax.experimental import pallas as pl
from jax.experimental.pallas import tpu as pltpu
from jax.sharding import PartitionSpec as P

ITERS = 3
RHO = 5.0
RIDGE = 0.25
LANES = 128
SUB = 8
PIECES = 3
MESH = pl.DeviceIdType.MESH


def cmul(a, b):
    return (a[0] * b[0] - a[1] * b[1], a[0] * b[1] + a[1] * b[0])


def cmul_conj(a, b):
    return (a[0] * b[0] + a[1] * b[1], a[1] * b[0] - a[0] * b[1])


def cadd(a, b):
    return (a[0] + b[0], a[1] + b[1])


def conj(a):
    return (a[0], -a[1])


def re_mul(a, b):
    return a[0] * b[0] - a[1] * b[1]


def scale(r, a):
    return (r * a[0], r * a[1])


def split_store(ref, rows, value):
    left = value
    for piece in range(PIECES):
        part = left.astype(jnp.bfloat16)
        ref[piece * rows : (piece + 1) * rows, :] = part
        if piece + 1 < PIECES:
            left = left - part.astype(jnp.float32)


def join(value, rows):
    total = value[0:rows]
    for piece in range(1, PIECES):
        total = total + value[piece * rows : (piece + 1) * rows]
    return total


def kernel(
    n_band, n_dir, dirs, times, base, stations,
    vis, coh, jones0, dual0, cons0, row, ids_row, ids_col,
    jones, dual, coeffs,
    cons, xall, rows_all, weights, gweights,
    gather_hot, scatter_hot, lhs, lhs_n, ends, grams, cross, vals, vals_n, seg, seg_n,
    model, got_a, sum_a, got_b, sum_b, got_c, res,
    row_send, row_recv, x_send, x_recv, d_send, d_recv,
):
    f32 = jnp.float32
    nrow = 8 * dirs
    per = stations // LANES
    me = lax.axis_index("band")
    mine = lax.axis_index("dir")
    blocks = base // LANES
    halves = times // SUB
    stages = n_dir.bit_length() - 1

    def at(pos):
        half = pos // (n_band // 2)
        return (1 - half) * (2 * pos) + half * (2 * (n_band - 1 - pos) + 1)

    odd = lax.rem(me, 2)
    pos = (1 - odd) * (me // 2) + odd * (n_band - 1 - me // 2)
    nexts = (at(lax.rem(pos + 1, n_band)), at(lax.rem(pos + n_band - 1, n_band)))

    def flip(stage):
        bit = lax.rem(mine // (1 << stage), 2)
        return mine + (1 - 2 * bit) * (1 << stage)

    own = lax.rem(mine, 2)

    barrier = pltpu.get_barrier_semaphore()
    for step in range(1, n_band):
        pl.semaphore_signal(
            barrier, inc=1, device_id={"band": lax.rem(me + step, n_band)}, device_id_type=MESH
        )
    for stage in range(stages):
        pl.semaphore_signal(barrier, inc=1, device_id={"dir": flip(stage)}, device_id_type=MESH)

    step_rows = 32

    def hot_body(i, carry):
        start = pl.multiple_of(i * step_rows, step_rows)
        for j in range(2 * base // LANES):
            lane = slice(j * LANES, (j + 1) * LANES)
            sid = lax.broadcasted_iota(jnp.int32, (step_rows, LANES), 0) + i * step_rows
            same = sid == jnp.broadcast_to(ids_row[0:1, lane], (step_rows, LANES))
            gather_hot[pl.ds(start, step_rows), lane] = jnp.where(same, 1.0, 0.0).astype(jnp.bfloat16)
        return carry

    lax.fori_loop(0, stations // step_rows, hot_body, 0)

    def hot_body2(i, carry):
        start = pl.multiple_of(i * step_rows, step_rows)
        col = ids_col[pl.ds(start, step_rows), :]
        for j in range(stations // LANES):
            lane = slice(j * LANES, (j + 1) * LANES)
            sid = lax.broadcasted_iota(jnp.int32, (step_rows, LANES), 1) + j * LANES
            scatter_hot[pl.ds(start, step_rows), lane] = jnp.where(sid == col, 1.0, 0.0).astype(jnp.bfloat16)
        return carry

    lax.fori_loop(0, 2 * base // step_rows, hot_body2, 0)

    pl.semaphore_wait(barrier, n_band - 1 + stages)

    row_copies = []
    for step in range(1, n_band):
        copy = pltpu.make_async_remote_copy(
            src_ref=row,
            dst_ref=rows_all.at[step],
            send_sem=row_send.at[step],
            recv_sem=row_recv.at[step],
            device_id={"band": lax.rem(me + step, n_band)},
            device_id_type=MESH,
        )
        copy.start()
        row_copies.append(copy)

    cons[...] = cons0[...]
    dual[...] = dual0[...]

    pairs = [(a, b) for a in range(4) for b in range(a, 4)]

    def gram_body(j, carry):
        lane = pl.ds(pl.multiple_of(j * LANES, LANES), LANES)
        for k in range(dirs):
            c = [
                [coh[k, v, h * SUB : (h + 1) * SUB, lane] for h in range(halves)]
                for v in range(8)
            ]
            for n, (a, b) in enumerate(pairs):
                real = sum(c[a][h] * c[b][h] + c[4 + a][h] * c[4 + b][h] for h in range(halves))
                grams[(2 * n) * dirs + k : (2 * n) * dirs + k + 1, lane] = jnp.sum(real, axis=0, keepdims=True)
                if a != b:
                    imag = sum(c[4 + a][h] * c[b][h] - c[a][h] * c[4 + b][h] for h in range(halves))
                    grams[(2 * n + 1) * dirs + k : (2 * n + 1) * dirs + k + 1, lane] = jnp.sum(
                        imag, axis=0, keepdims=True
                    )
        return carry

    lax.fori_loop(0, blocks, gram_body, 0)

    def gram(a, b):
        if a > b:
            return conj(gram(b, a))
        n = pairs.index((a, b))
        real = grams[(2 * n) * dirs : (2 * n + 1) * dirs, :]
        if a == b:
            return real
        return (real, grams[(2 * n + 1) * dirs : (2 * n + 2) * dirs, :])

    def solve_weights():
        for copy in row_copies:
            copy.wait()
        rows_all[0] = row[...]
        held = [rows_all[s] for s in range(n_band)]
        columns = []
        for m in range(SUB):
            total = held[0] * held[0][m : m + 1, :]
            for s in range(1, n_band):
                total = total + held[s] * held[s][m : m + 1, :]
            ident = jnp.where(lax.broadcasted_iota(jnp.int32, (SUB, LANES), 0) == m, RIDGE * n_band, 0.0)
            columns.append(total + ident.astype(f32))
        right = list(held)
        iota = lax.broadcasted_iota(jnp.int32, (SUB, LANES), 0)
        for i in range(SUB):
            inverse = 1.0 / columns[i][i : i + 1, :]
            factor = columns[i]
            for group in (columns, right):
                for c in range(len(group)):
                    lead = jnp.broadcast_to(group[c][i : i + 1, :] * inverse, (SUB, LANES))
                    group[c] = jnp.where(iota == i, lead, group[c] - factor * lead)
        for s in range(n_band):
            band = lax.rem(me + n_band - s, n_band)
            gweights[band] = right[s]
            weights[band] = jnp.broadcast_to(
                jnp.sum(right[s] * held[0], axis=0, keepdims=True), (SUB, LANES)
            )

    x_copies = [{} for _ in range(ITERS)]

    def send_x(turn, k, slot):
        copy = pltpu.make_async_remote_copy(
            src_ref=xall.at[turn, k, slot],
            dst_ref=xall.at[turn, k, slot + 1],
            send_sem=x_send.at[turn, k, slot],
            recv_sem=x_recv.at[turn, k, slot],
            device_id={"band": nexts[k % 2]},
            device_id_type=MESH,
        )
        copy.start()
        x_copies[turn][(k, slot)] = copy

    def pump(turn, slot):
        for k in range(dirs):
            x_copies[turn][(k, slot - 1)].wait_recv()
            if slot < n_band - 1:
                send_x(turn, k, slot)

    def source(k, slot):
        if k % 2 == 0:
            return at(lax.rem(pos + n_band - slot, n_band))
        return at(lax.rem(pos + slot, n_band))

    def end(comp, lane):
        return ends[comp * dirs : (comp + 1) * dirs, lane]

    d_copies = []

    def send_d(turn, n, src, dst, stage):
        copy = pltpu.make_async_remote_copy(
            src_ref=src,
            dst_ref=dst,
            send_sem=d_send.at[turn, n],
            recv_sem=d_recv.at[turn, n],
            device_id={"dir": flip(stage)},
            device_id_type=MESH,
        )
        copy.start()
        d_copies.append(copy)
        return copy

    first = slice(0, base)
    second = slice(base, 2 * base)

    for turn in range(ITERS):
        start_ref = jones0 if turn == 0 else jones
        for g in range(nrow // SUB):
            for j in range(per):
                value = start_ref[pl.ds(g * SUB * per + j, SUB, stride=per), :]
                left = value
                for piece in range(PIECES):
                    part = left.astype(jnp.bfloat16)
                    lhs[
                        piece * nrow + g * SUB : piece * nrow + (g + 1) * SUB,
                        j * LANES : (j + 1) * LANES,
                    ] = part
                    left = left - part.astype(f32)
        ends[...] = join(jnp.dot(lhs[...], gather_hot[...], preferred_element_type=f32), nrow)

        def model_body(i, carry):
            j = i // halves
            h = lax.rem(i, halves)
            lane = pl.ds(pl.multiple_of(j * LANES, LANES), LANES)
            lane_q = pl.ds(pl.multiple_of(base + j * LANES, LANES), LANES)
            time = pl.ds(pl.multiple_of(h * SUB, SUB), SUB)
            total = [None] * 4
            for k in range(dirs):
                c = [(coh[k, v, time, lane], coh[k, 4 + v, time, lane]) for v in range(4)]

                def spread(v, where):
                    return tuple(
                        jnp.broadcast_to(
                            ends[(4 * part + v) * dirs + k : (4 * part + v) * dirs + k + 1, where],
                            (SUB, LANES),
                        )
                        for part in range(2)
                    )

                p = [spread(v, lane) for v in range(4)]
                q = [spread(v, lane_q) for v in range(4)]
                for a in range(2):
                    b = [cadd(cmul(p[2 * a], c[d]), cmul(p[2 * a + 1], c[2 + d])) for d in range(2)]
                    for d in range(2):
                        term = cadd(cmul_conj(b[0], q[2 * d]), cmul_conj(b[1], q[2 * d + 1]))
                        v = 2 * a + d
                        total[v] = term if total[v] is None else cadd(total[v], term)
            for v in range(4):
                model[turn, 0, v, time, lane] = total[v][0]
                model[turn, 1, v, time, lane] = total[v][1]
            return carry

        lax.fori_loop(0, blocks * halves, model_body, 0)

        other = 1 - own
        hop = send_d(turn, 0, model.at[turn, other], got_a.at[turn], 0)
        if turn > 0:
            pump(turn - 1, 1)

        jp = [(end(v, first), end(4 + v, first)) for v in range(4)]
        jq = [(end(v, second), end(4 + v, second)) for v in range(4)]

        def gram_of(j):
            m00 = re_mul(j[0], conj(j[0])) + re_mul(j[2], conj(j[2]))
            m11 = re_mul(j[1], conj(j[1])) + re_mul(j[3], conj(j[3]))
            m01 = cadd(cmul_conj(j[1], j[0]), cmul_conj(j[3], j[2]))
            return m00, m11, m01

        m00, m11, m01 = gram_of(jq)
        p00, p11, p01 = gram_of(jp)
        n1_00 = m00 * gram(0, 0) + m11 * gram(1, 1) + 2.0 * re_mul(m01, gram(0, 1))
        n1_11 = m00 * gram(2, 2) + m11 * gram(3, 3) + 2.0 * re_mul(m01, gram(2, 3))
        n1_01 = cadd(
            cadd(scale(m00, gram(0, 2)), scale(m11, gram(1, 3))),
            cadd(cmul(m01, gram(0, 3)), cmul(conj(m01), gram(1, 2))),
        )
        n2_00 = p00 * gram(0, 0) + p11 * gram(2, 2) + 2.0 * re_mul(p01, gram(2, 0))
        n2_11 = p00 * gram(1, 1) + p11 * gram(3, 3) + 2.0 * re_mul(p01, gram(3, 1))
        n2_01 = cadd(
            cadd(scale(p00, gram(1, 0)), scale(p11, gram(3, 2))),
            cadd(cmul(p01, gram(3, 0)), cmul(conj(p01), gram(1, 2))),
        )
        for n, (left, right) in enumerate(
            ((n1_00, n2_00), (n1_11, n2_11), (n1_01[0], n2_01[0]), (n1_01[1], n2_01[1]))
        ):
            vals_n[n * dirs : (n + 1) * dirs, first] = left
            vals_n[n * dirs : (n + 1) * dirs, second] = right

        hop.wait_recv()
        sum_a[turn, 0] = model[turn, own] + got_a[turn]
        for stage in range(1, stages):
            hop = send_d(turn, stage, sum_a.at[turn, stage - 1], got_b.at[turn, stage - 1], stage)
            if stage == 1:
                split_store(lhs_n, 4 * dirs, vals_n[...])
                found = join(jnp.dot(lhs_n[...], scatter_hot[...], preferred_element_type=f32), 4 * dirs)
                for g in range(4 * dirs // SUB):
                    for j in range(per):
                        seg_n[pl.ds(g * SUB * per + j, SUB, stride=per), :] = found[
                            g * SUB : (g + 1) * SUB, j * LANES : (j + 1) * LANES
                        ]
                if turn == 0:
                    solve_weights()
                else:
                    for s in range(2, n_band // 2):
                        pump(turn - 1, s)
            hop.wait_recv()
            target = sum_a.at[turn, stage] if stage + 1 < stages else sum_b.at[turn]
            target[...] = sum_a[turn, stage - 1] + got_b[turn, stage - 1]
        hop = send_d(turn, stages, sum_b.at[turn], got_c.at[turn], 0)
        if turn > 0:
            pump(turn - 1, n_band // 2)
        res[own] = vis[own] - sum_b[turn]
        hop.wait_recv()
        res[other] = vis[other] - got_c[turn]

        def cross_body(j, carry):
            lane = pl.ds(pl.multiple_of(j * LANES, LANES), LANES)
            r = [[res[v // 4, v % 4, h * SUB : (h + 1) * SUB, lane] for h in range(halves)] for v in range(8)]
            for k in range(dirs):
                c = [[coh[k, v, h * SUB : (h + 1) * SUB, lane] for h in range(halves)] for v in range(8)]
                for a in range(4):
                    for b in range(4):
                        real = sum(r[a][h] * c[b][h] + r[4 + a][h] * c[4 + b][h] for h in range(halves))
                        imag = sum(r[4 + a][h] * c[b][h] - r[a][h] * c[4 + b][h] for h in range(halves))
                        n = 2 * (4 * a + b)
                        cross[n * dirs + k : n * dirs + k + 1, lane] = jnp.sum(real, axis=0, keepdims=True)
                        cross[(n + 1) * dirs + k : (n + 1) * dirs + k + 1, lane] = jnp.sum(
                            imag, axis=0, keepdims=True
                        )
            return carry

        lax.fori_loop(0, blocks, cross_body, 0)

        if turn > 0:
            for s in range(n_band // 2 + 1, n_band - 1):
                pump(turn - 1, s)

        def crossed(a, b):
            n = 2 * (4 * a + b)
            return (
                cross[n * dirs : (n + 1) * dirs, :],
                cross[(n + 1) * dirs : (n + 2) * dirs, :],
            )

        def herm(which):
            zero = [vals_n[n * dirs : (n + 1) * dirs, which] for n in range(4)]
            return zero[0], zero[1], (zero[2], zero[3])

        for which, j, other_end in ((first, jq, jp), (second, jp, jq)):
            h00, h11, h01 = herm(which)
            for a in range(2):
                for c in range(2):
                    total = None
                    for b in range(2):
                        for d in range(2):
                            if which is first:
                                term = cmul(j[2 * b + d], crossed(2 * a + b, 2 * c + d))
                            else:
                                term = cmul_conj(j[2 * b + d], crossed(2 * b + a, 2 * d + c))
                            total = term if total is None else cadd(total, term)
                    if c == 0:
                        extra = cadd(scale(h00, other_end[2 * a]), cmul_conj(other_end[2 * a + 1], h01))
                    else:
                        extra = cadd(cmul(other_end[2 * a], h01), scale(h11, other_end[2 * a + 1]))
                    total = cadd(total, extra)
                    for part in range(2):
                        n = 4 * part + 2 * a + c
                        vals[n * dirs : (n + 1) * dirs, which] = total[part]

        split_store(lhs, nrow, vals[...])
        found = join(jnp.dot(lhs[...], scatter_hot[...], preferred_element_type=f32), nrow)
        for g in range(nrow // SUB):
            for j in range(per):
                seg[pl.ds(g * SUB * per + j, SUB, stride=per), :] = found[
                    g * SUB : (g + 1) * SUB, j * LANES : (j + 1) * LANES
                ]

        def join_bands(previous):
            pump(previous, n_band - 1)
            for k in range(dirs):
                for v in range(8):
                    here = pl.ds((v * dirs + k) * per, per)
                    total = None
                    for s in range(n_band):
                        term = weights[source(k, s)] * xall[previous, k, s, v]
                        total = term if total is None else total + term
                    cons[here, :] = total
                    dual[here, :] = dual[here, :] + RHO * (jones[here, :] - total)

        if turn > 0:
            join_bands(turn - 1)

        for k in range(dirs):
            def rows_of(v):
                return pl.ds((v * dirs + k) * per, per)

            y = []
            for v in range(8):
                here = rows_of(v)
                y.append(seg[here, :] + RHO * cons[here, :] - dual[here, :])
            h00, h11, re01, im01 = [seg_n[rows_of(n), :] for n in range(4)]
            h00 = h00 + RHO
            h11 = h11 + RHO
            inverse = 1.0 / (h00 * h11 - (re01 * re01 + im01 * im01))
            h00, h11, h01 = h00 * inverse, h11 * inverse, (re01 * inverse, im01 * inverse)
            for a in range(2):
                y0, y1 = (y[2 * a], y[4 + 2 * a]), (y[2 * a + 1], y[4 + 2 * a + 1])
                minus0, minus1 = cmul_conj(y1, h01), cmul(y0, h01)
                for part in range(2):
                    for c in range(2):
                        if c == 0:
                            value = h11 * y0[part] - minus0[part]
                        else:
                            value = h00 * y1[part] - minus1[part]
                        v = 4 * part + 2 * a + c
                        here = rows_of(v)
                        jones[here, :] = value
                        xall[turn, k, 0, v] = value + dual[here, :] * (1.0 / RHO)
            send_x(turn, k, 0)

    last = ITERS - 1
    for s in range(1, n_band - 1):
        pump(last, s)
    join_bands(last)

    def coeff_body(m, carry):
        for k in range(dirs):
            total = [None] * 8
            for s in range(n_band):
                factor = jnp.broadcast_to(gweights[source(k, s), pl.ds(m, 1), :], (SUB, LANES))
                for v in range(8):
                    term = factor * xall[last, k, s, v]
                    total[v] = term if total[v] is None else total[v] + term
            for v in range(8):
                coeffs[m, k, v] = total[v]
        return carry

    lax.fori_loop(0, SUB, coeff_body, 0)

    for copies in x_copies:
        for copy in copies.values():
            copy.wait_send()
    for copy in d_copies:
        copy.wait_send()


def local(n_band, n_dir, vis, coh, jones_start, dual_start, consensus_start, freq_basis, pairs):
    f32 = jnp.float32
    dirs, times, base = coh.shape[1], coh.shape[-2], coh.shape[-1]
    stations = jones_start.shape[-1]
    per = stations // LANES
    nrow = 8 * dirs
    terms = freq_basis.shape[1]

    def pack(value):
        value = value.reshape(dirs, 8, per, LANES)
        return jnp.swapaxes(value, 0, 1).reshape(nrow * per, LANES)

    def unpack(value):
        value = value.reshape(8, dirs, per, LANES)
        return jnp.swapaxes(value, 0, 1).reshape(jones_start.shape)

    row = freq_basis[0]
    cons0 = jnp.sum(row.reshape((terms,) + (1,) * 5) * consensus_start, axis=0)
    ids = pairs.reshape(-1)
    stages = n_dir.bit_length() - 1
    half = (4, times, base)
    vmem = pl.BlockSpec(memory_space=pltpu.VMEM)
    packed = jax.ShapeDtypeStruct((nrow * per, LANES), f32)
    bf16 = jnp.bfloat16
    jones, dual, coeffs = pl.pallas_call(
        functools.partial(kernel, n_band, n_dir, dirs, times, base, stations),
        out_shape=(packed, packed, jax.ShapeDtypeStruct((terms, dirs, 8, per, LANES), f32)),
        in_specs=[vmem] * 8,
        out_specs=(vmem,) * 3,
        scratch_shapes=[
            pltpu.VMEM((nrow * per, LANES), f32),
            pltpu.VMEM((ITERS, dirs, n_band, 8, per, LANES), f32),
            pltpu.VMEM((n_band, SUB, LANES), f32),
            pltpu.VMEM((n_band, SUB, LANES), f32),
            pltpu.VMEM((n_band, SUB, LANES), f32),
            pltpu.VMEM((stations, 2 * base), bf16),
            pltpu.VMEM((2 * base, stations), bf16),
            pltpu.VMEM((PIECES * nrow, max(stations, 2 * base)), bf16),
            pltpu.VMEM((PIECES * 4 * dirs, 2 * base), bf16),
            pltpu.VMEM((nrow, 2 * base), f32),
            pltpu.VMEM((20 * dirs, base), f32),
            pltpu.VMEM((32 * dirs, base), f32),
            pltpu.VMEM((nrow, 2 * base), f32),
            pltpu.VMEM((4 * dirs, 2 * base), f32),
            pltpu.VMEM((nrow * per, LANES), f32),
            pltpu.VMEM((4 * dirs * per, LANES), f32),
            pltpu.VMEM((ITERS, 2) + half, f32),
            pltpu.VMEM((ITERS,) + half, f32),
            pltpu.VMEM((ITERS, stages - 1) + half, f32),
            pltpu.VMEM((ITERS, stages - 1) + half, f32),
            pltpu.VMEM((ITERS,) + half, f32),
            pltpu.VMEM((ITERS,) + half, f32),
            pltpu.VMEM((2,) + half, f32),
            pltpu.SemaphoreType.DMA((n_band,)),
            pltpu.SemaphoreType.DMA((n_band,)),
            pltpu.SemaphoreType.DMA((ITERS, dirs, n_band - 1)),
            pltpu.SemaphoreType.DMA((ITERS, dirs, n_band - 1)),
            pltpu.SemaphoreType.DMA((ITERS, stages + 1)),
            pltpu.SemaphoreType.DMA((ITERS, stages + 1)),
        ],
        compiler_params=pltpu.CompilerParams(
            collective_id=0, has_side_effects=True, vmem_limit_bytes=60 * 1024 * 1024
        ),
    )(
        vis.reshape((2,) + half),
        coh.reshape(dirs, 8, times, base),
        pack(jones_start),
        pack(dual_start),
        pack(cons0),
        jnp.broadcast_to(row[:, None], (terms, LANES)),
        ids.reshape(1, -1),
        jnp.broadcast_to(ids[:, None], (2 * base, LANES)),
    )
    coeffs = coeffs.reshape(consensus_start.shape)
    return unpack(jones), unpack(dual), coeffs


def solution(mesh):
    in_specs = (
        P("band", None, None, None, None, None),
        P("band", "dir", None, None, None, None, None),
        P("band", "dir", None, None, None, None),
        P("band", "dir", None, None, None, None),
        P(None, "dir", None, None, None, None),
        P("band", None),
        P(),
    )
    out_specs = (
        P("band", "dir", None, None, None, None),
        P("band", "dir", None, None, None, None),
        P(None, "dir", None, None, None, None),
    )
    body = functools.partial(local, mesh.shape["band"], mesh.shape["dir"])
    return jax.shard_map(body, mesh=mesh, in_specs=in_specs, out_specs=out_specs, check_vma=False)
```

time: 548 us -> 102 us (0.19); the launches traced: 538 us -> 102 us
  waiting for transfers between devices: 265 us -> 0 us
  local copies, waits for them, and re-layouts: 155 us -> 14.1 us
  Pallas kernels: 0 us -> 86.6 us
  other arithmetic: 56.7 us -> 0.61 us
  blocking collectives: 23.1 us -> 0 us
  matrix products: 20.7 us -> 0 us
  between operations: 16.6 us -> 0.69 us
    psum x6 -> x0, waiting for transfers between devices: 265 us -> none  [the longest x3 224 us: local(): coeff_sums = lax.psum(local_terms, 'band')]
    pallas_call x0 -> x1, Pallas kernels: none -> 86.6 us  [local(): pl.pallas_call(functools.partial(kernel, n_band, n_dir, dirs, times, base...]
    mul x92 -> x0, local copies, waits for them, and re-layouts: 57.9 us -> none  [small_mul(): return left[:, 0:1] * right[0:1] + left[:, 1:2] * right[1:2]]
    gather x6 -> x0, local copies, waits for them, and re-layouts: 42.8 us -> none  [the longest x3 21.4 us: predict(): jones_second = jnp.take(jones_k, second, axis=-1)[..., None, :]]
    psum x1 -> x0, blocking collectives: 23.1 us -> none  [local(): lax.psum(outer, 'band')]
    sub x27 -> x0, other arithmetic: 20.1 us -> none  [the longest x21 15.8 us: complex_mul(): real_part = small_mul(left[0], right[0]) - small_mul(left[1], right[1])]
    slice x11 -> x0, local copies, waits for them, and re-layouts: 17.2 us -> none  [the longest x10 16.4 us: small_mul(): return left[:, 0:1] * right[0:1] + left[:, 1:2] * right[1:2]]
    broadcast_in_dim x8 -> x0, other arithmetic: 16.6 us -> none  [the longest x3 9.07 us: predict(): jones_first = jnp.take(jones_k, first, axis=-1)[..., None, :]]
  transfers between devices with their start and end apart: 6 -> 0, of which waited for: 5 -> 0; matrix products, arithmetic and copies ran while one was open for 10% -> 0% of each run, Pallas kernels for 0% -> 0%
where the time goes in v1:
time: 102 us
  Pallas kernels  86.6 us (85%)
  local copies, waits for them, and re-layouts  14.1 us (14%)
    pallas_call x1, Pallas kernels, local(): pl.pallas_call(functools.partial(kernel, n_band, n_dir, dirs, times, base...  86.6 us
    reshape x6, local copies, waits for them, and re-layouts, pack(): value = value.reshape(dirs, 8, per, LANES)  4.11 us
    reshape x4, local copies, waits for them, and re-layouts, unpack(): return jnp.swapaxes(value, 0, 1).reshape(jones_start.shape)  3.5 us
    unnamed x8, local copies, waits for them, and re-layouts  2.63 us

profile of v1, /device:TPU:0, one launch (start us, length us, event | category | flops | bytes accessed | tf_op | source)
XLA Modules:
  0.0 102.0 jit_solution(1302079613211699755)
XLA Ops:
  0.6 0.0 copy-start
  0.6 1.4 %broadcast_in_dim.12.row = f32[8,128]{1,0:T(8,128)} broadcast(f32[8]{0:T(128)} %bitcast.44), dimensions={0} | broadcast | bytes 4128 | tf_op jit(solution)/shard_map/broadcast_in_dim | solution.py:555
  2.0 1.3 %copy.21 = s32[1,1,2,512]{3,1,2,0:T(1,128)} copy(s32[1,1,2,512]{3,2,1,0:T(2,128)} %bitcast.42) | data formatting | bytes 8192
  3.3 0.7 copy.22
  4.0 1.0 reshape.50
  5.0 0.7 copy.14
  5.7 1.0 reshape.52
  6.7 0.7 copy.15
  7.4 0.0 copy-start.2
  7.4 0.0 copy-done
  7.4 0.7 copy-done.2
  8.0 0.6 multiply_reduce_fusion
  8.6 0.1 reshape.54
  8.8 0.7 copy.16
  9.4 1.0 broadcast_in_dim.14.ids_col
  10.4 86.6 %shard_map.94 = (f32[256,128]{1,0:T(8,128)}, f32[256,128]{1,0:T(8,128)}, f32[8,4,8,8,128]{4,3,2,1,0:T(8,128)}) custom-call(f32[2,4,16,512]{3,2,1,0:T(8,128)} %bitcast.37, f32[4,8,16,512]{3,2,1,0:T(8,128)} %bitcast.33, f32[256,128]{1,0:T(8,128)} %bitcast.34, f32[256,128]{1,0:T(8,128)} %bitcast.35, f32[256,128]{1,0:T(8,128)} %bitcast.36, ...), custom_call_target="tpu_custom_call" | custom-call | tf_op jit(solution)/shard_map/pallas_call | solution.py:510
  97.0 0.0 copy-start.1
  97.0 1.0 %reshape.61 = f32[1,4,2,2,2,1024]{5,1,4,3,2,0:T(4,128)S(1)} reshape(f32[4,8,8,128]{3,2,0,1:T(8,128)} %bitcast.39) | data formatting | bytes 262144 | tf_op jit(solution)/shard_map/reshape | solution.py:500
  98.0 0.8 copy.19
  98.8 0.9 reshape.62
  99.7 0.8 copy.20
  100.5 0.0 copy-done.1
  100.5 1.5 %reshape.60 = f32[8,4,2,2,2,1024]{5,4,3,2,1,0:T(2,128)} reshape(f32[8,4,8,8,128]{4,3,2,1,0:T(8,128)S(1)} %copy-done.1) | data formatting | bytes 2097152 | tf_op jit(solution)/shard_map/reshape | solution.py:559
Async XLA Ops:
  0.6 6.7 %copy-start = (f32[8,4,2,2,2,1024]{5,4,3,2,1,0:T(2,128)S(1)}, f32[8,4,2,2,2,1024]{5,4,3,2,1,0:T(2,128)}, u32[]{:S(2)}) copy-start(f32[8,4,2,2,2,1024]{5,4,3,2,1,0:T(2,128)} %param.11) | copy-start | bytes 3145732
  7.4 0.7 copy-start.2
  97.0 3.5 %copy-start.1 = (f32[8,4,8,8,128]{4,3,2,1,0:T(8,128)S(1)}, f32[8,4,8,8,128]{4,3,2,1,0:T(8,128)}, u32[]{:S(2)}) copy-start(f32[8,4,8,8,128]{4,3,2,1,0:T(8,128)} %get-tuple-element.8) | copy-start | bytes 3145732

commit v2 on v1

--- a/solution.py
+++ b/solution.py
@@ -58,12 +58,13 @@
 
 def kernel(
     n_band, n_dir, dirs, times, base, stations,
-    vis, coh, jones0, dual0, cons0, row, ids_row, ids_col,
-    jones, dual, coeffs,
+    vis_far, coh_far, jones0, dual0, coeffs0_far, basis, pairs_ref,
+    jones_out, dual_out, coeffs,
+    vis, coh, coeffs0, jones, dual, row, ids_col,
     cons, xall, rows_all, weights, gweights,
     gather_hot, scatter_hot, lhs, lhs_n, ends, grams, cross, vals, vals_n, seg, seg_n,
     model, got_a, sum_a, got_b, sum_b, got_c, res,
-    row_send, row_recv, x_send, x_recv, d_send, d_recv,
+    load_sem, row_send, row_recv, x_send, x_recv, d_send, d_recv,
 ):
     f32 = jnp.float32
     nrow = 8 * dirs
@@ -88,6 +89,11 @@
 
     own = lax.rem(mine, 2)
 
+    loads = []
+    for n, (far, near) in enumerate(((coh_far, coh), (vis_far, vis), (coeffs0_far, coeffs0))):
+        loads.append(pltpu.make_async_copy(far, near, load_sem.at[n]))
+        loads[-1].start()
+
     barrier = pltpu.get_barrier_semaphore()
     for step in range(1, n_band):
         pl.semaphore_signal(
@@ -96,6 +102,25 @@
     for stage in range(stages):
         pl.semaphore_signal(barrier, inc=1, device_id={"dir": flip(stage)}, device_id_type=MESH)
 
+    def halves_of(k, v):
+        return (k, v // 2, pl.ds(v % 2, per, stride=2), slice(None))
+
+    def packed(k, v):
+        return pl.ds((v * dirs + k) * per, per)
+
+    row[...] = jnp.zeros((SUB, LANES), f32)
+    for m in range(SUB):
+        row[m : m + 1, :] = jnp.full((1, LANES), basis[0, m], f32)
+    for k in range(dirs):
+        for v in range(8):
+            jones[packed(k, v), :] = jones0[halves_of(k, v)]
+            dual[packed(k, v), :] = dual0[halves_of(k, v)]
+
+    for j in range(2 * base // LANES):
+        lane = (j * LANES) % base
+        which = (j * LANES) // base
+        ids = jnp.broadcast_to(pairs_ref[which : which + 1, lane : lane + LANES], (LANES, LANES))
+        ids_col[j * LANES : (j + 1) * LANES, :] = jnp.transpose(ids)
     step_rows = 32
 
     def hot_body(i, carry):
@@ -103,7 +128,9 @@
         for j in range(2 * base // LANES):
             lane = slice(j * LANES, (j + 1) * LANES)
             sid = lax.broadcasted_iota(jnp.int32, (step_rows, LANES), 0) + i * step_rows
-            same = sid == jnp.broadcast_to(ids_row[0:1, lane], (step_rows, LANES))
+            which, low = (j * LANES) // base, (j * LANES) % base
+            ids = pairs_ref[which : which + 1, low : low + LANES]
+            same = sid == jnp.broadcast_to(ids, (step_rows, LANES))
             gather_hot[pl.ds(start, step_rows), lane] = jnp.where(same, 1.0, 0.0).astype(jnp.bfloat16)
         return carry
 
@@ -135,8 +162,7 @@
         copy.start()
         row_copies.append(copy)
 
-    cons[...] = cons0[...]
-    dual[...] = dual0[...]
+    loads[0].wait()
 
     pairs = [(a, b) for a in range(4) for b in range(a, 4)]
 
@@ -167,6 +193,16 @@
         if a == b:
             return real
         return (real, grams[(2 * n + 1) * dirs : (2 * n + 2) * dirs, :])
+
+    def start_consensus():
+        loads[1].wait()
+        loads[2].wait()
+        for k in range(dirs):
+            for v in range(8):
+                total = basis[0, 0] * coeffs0[(0,) + halves_of(k, v)]
+                for m in range(1, SUB):
+                    total = total + basis[0, m] * coeffs0[(m,) + halves_of(k, v)]
+                cons[packed(k, v), :] = total
 
     def solve_weights():
         for copy in row_copies:
@@ -198,28 +234,37 @@
 
     x_copies = [{} for _ in range(ITERS)]
 
-    def send_x(turn, k, slot):
+    ahead = n_band // 2
+    behind = n_band - 1 - ahead
+
+    def slot_of(way, distance):
+        return distance if way == 0 or distance == 0 else ahead + distance
+
+    def send_x(turn, k, way, distance):
+        to = slot_of(way, distance + 1)
         copy = pltpu.make_async_remote_copy(
-            src_ref=xall.at[turn, k, slot],
-            dst_ref=xall.at[turn, k, slot + 1],
-            send_sem=x_send.at[turn, k, slot],
-            recv_sem=x_recv.at[turn, k, slot],
-            device_id={"band": nexts[k % 2]},
+            src_ref=xall.at[turn, k, slot_of(way, distance)],
+            dst_ref=xall.at[turn, k, to],
+            send_sem=x_send.at[turn, k, to - 1],
+            recv_sem=x_recv.at[turn, k, to - 1],
+            device_id={"band": nexts[way]},
             device_id_type=MESH,
         )
         copy.start()
-        x_copies[turn][(k, slot)] = copy
-
-    def pump(turn, slot):
+        x_copies[turn][(k, way, distance + 1)] = copy
+
+    def pump(turn, distance):
         for k in range(dirs):
-            x_copies[turn][(k, slot - 1)].wait_recv()
-            if slot < n_band - 1:
-                send_x(turn, k, slot)
-
-    def source(k, slot):
-        if k % 2 == 0:
+            for way, reach in enumerate((ahead, behind)):
+                if distance <= reach:
+                    x_copies[turn][(k, way, distance)].wait_recv()
+                    if distance < reach:
+                        send_x(turn, k, way, distance)
+
+    def source(slot):
+        if slot <= ahead:
             return at(lax.rem(pos + n_band - slot, n_band))
-        return at(lax.rem(pos + slot, n_band))
+        return at(lax.rem(pos + slot - ahead, n_band))
 
     def end(comp, lane):
         return ends[comp * dirs : (comp + 1) * dirs, lane]
@@ -243,10 +288,9 @@
     second = slice(base, 2 * base)
 
     for turn in range(ITERS):
-        start_ref = jones0 if turn == 0 else jones
         for g in range(nrow // SUB):
             for j in range(per):
-                value = start_ref[pl.ds(g * SUB * per + j, SUB, stride=per), :]
+                value = jones[pl.ds(g * SUB * per + j, SUB, stride=per), :]
                 left = value
                 for piece in range(PIECES):
                     part = left.astype(jnp.bfloat16)
@@ -338,16 +382,18 @@
                             g * SUB : (g + 1) * SUB, j * LANES : (j + 1) * LANES
                         ]
                 if turn == 0:
+                    start_consensus()
                     solve_weights()
                 else:
-                    for s in range(2, n_band // 2):
+                    for s in range(2, (ahead + 2) // 2):
                         pump(turn - 1, s)
             hop.wait_recv()
             target = sum_a.at[turn, stage] if stage + 1 < stages else sum_b.at[turn]
             target[...] = sum_a[turn, stage - 1] + got_b[turn, stage - 1]
         hop = send_d(turn, stages, sum_b.at[turn], got_c.at[turn], 0)
         if turn > 0:
-            pump(turn - 1, n_band // 2)
+            for s in range(max(2, (ahead + 2) // 2), ahead):
+                pump(turn - 1, s)
         res[own] = vis[own] - sum_b[turn]
         hop.wait_recv()
         res[other] = vis[other] - got_c[turn]
@@ -369,10 +415,6 @@
             return carry
 
         lax.fori_loop(0, blocks, cross_body, 0)
-
-        if turn > 0:
-            for s in range(n_band // 2 + 1, n_band - 1):
-                pump(turn - 1, s)
 
         def crossed(a, b):
             n = 2 * (4 * a + b)
@@ -415,16 +457,20 @@
                 ]
 
         def join_bands(previous):
-            pump(previous, n_band - 1)
+            pump(previous, ahead)
             for k in range(dirs):
                 for v in range(8):
                     here = pl.ds((v * dirs + k) * per, per)
                     total = None
                     for s in range(n_band):
-                        term = weights[source(k, s)] * xall[previous, k, s, v]
+                        term = weights[source(s)] * xall[previous, k, s, v]
                         total = term if total is None else total + term
                     cons[here, :] = total
-                    dual[here, :] = dual[here, :] + RHO * (jones[here, :] - total)
+                    fresh = dual[here, :] + RHO * (jones[here, :] - total)
+                    if previous + 1 < ITERS:
+                        dual[here, :] = fresh
+                    else:
+                        dual_out[halves_of(k, v)] = fresh
 
         if turn > 0:
             join_bands(turn - 1)
@@ -454,11 +500,15 @@
                         v = 4 * part + 2 * a + c
                         here = rows_of(v)
                         jones[here, :] = value
+                        if turn + 1 == ITERS:
+                            jones_out[halves_of(k, v)] = value
                         xall[turn, k, 0, v] = value + dual[here, :] * (1.0 / RHO)
-            send_x(turn, k, 0)
+            for way, reach in enumerate((ahead, behind)):
+                if reach:
+                    send_x(turn, k, way, 0)
 
     last = ITERS - 1
-    for s in range(1, n_band - 1):
+    for s in range(1, ahead):
         pump(last, s)
     join_bands(last)
 
@@ -466,12 +516,12 @@
         for k in range(dirs):
             total = [None] * 8
             for s in range(n_band):
-                factor = jnp.broadcast_to(gweights[source(k, s), pl.ds(m, 1), :], (SUB, LANES))
+                factor = jnp.broadcast_to(gweights[source(s), pl.ds(m, 1), :], (SUB, LANES))
                 for v in range(8):
                     term = factor * xall[last, k, s, v]
                     total[v] = term if total[v] is None else total[v] + term
             for v in range(8):
-                coeffs[m, k, v] = total[v]
+                coeffs[(m,) + halves_of(k, v)] = total[v]
         return carry
 
     lax.fori_loop(0, SUB, coeff_body, 0)
@@ -491,28 +541,35 @@
     nrow = 8 * dirs
     terms = freq_basis.shape[1]
 
-    def pack(value):
-        value = value.reshape(dirs, 8, per, LANES)
-        return jnp.swapaxes(value, 0, 1).reshape(nrow * per, LANES)
-
-    def unpack(value):
-        value = value.reshape(8, dirs, per, LANES)
-        return jnp.swapaxes(value, 0, 1).reshape(jones_start.shape)
-
-    row = freq_basis[0]
-    cons0 = jnp.sum(row.reshape((terms,) + (1,) * 5) * consensus_start, axis=0)
-    ids = pairs.reshape(-1)
+    def enter(value):
+        lead = value.shape[:-2]
+        value = value.reshape(lead + (2, per, LANES))
+        return jnp.swapaxes(value, -2, -3).reshape(lead + (2 * per, LANES))
+
+    def leave(value, shape):
+        value = value.reshape(value.shape[:-2] + (per, 2, LANES))
+        return jnp.swapaxes(value, -2, -3).reshape(shape)
+
     stages = n_dir.bit_length() - 1
     half = (4, times, base)
     vmem = pl.BlockSpec(memory_space=pltpu.VMEM)
-    packed = jax.ShapeDtypeStruct((nrow * per, LANES), f32)
+    far = pl.BlockSpec(memory_space=pl.ANY)
+    raw = (dirs, 4, 2 * per, LANES)
+    raw_out = jax.ShapeDtypeStruct(raw, f32)
     bf16 = jnp.bfloat16
     jones, dual, coeffs = pl.pallas_call(
         functools.partial(kernel, n_band, n_dir, dirs, times, base, stations),
-        out_shape=(packed, packed, jax.ShapeDtypeStruct((terms, dirs, 8, per, LANES), f32)),
-        in_specs=[vmem] * 8,
+        out_shape=(raw_out, raw_out, jax.ShapeDtypeStruct((terms,) + raw, f32)),
+        in_specs=[far, far, vmem, vmem, far, pl.BlockSpec(memory_space=pltpu.SMEM), vmem],
         out_specs=(vmem,) * 3,
         scratch_shapes=[
+            pltpu.VMEM((2,) + half, f32),
+            pltpu.VMEM((dirs, 8, times, base), f32),
+            pltpu.VMEM((terms,) + raw, f32),
+            pltpu.VMEM((nrow * per, LANES), f32),
+            pltpu.VMEM((nrow * per, LANES), f32),
+            pltpu.VMEM((SUB, LANES), f32),
+            pltpu.VMEM((2 * base, LANES), jnp.int32),
             pltpu.VMEM((nrow * per, LANES), f32),
             pltpu.VMEM((ITERS, dirs, n_band, 8, per, LANES), f32),
             pltpu.VMEM((n_band, SUB, LANES), f32),
@@ -536,6 +593,7 @@
             pltpu.VMEM((ITERS,) + half, f32),
             pltpu.VMEM((ITERS,) + half, f32),
             pltpu.VMEM((2,) + half, f32),
+            pltpu.SemaphoreType.DMA((3,)),
             pltpu.SemaphoreType.DMA((n_band,)),
             pltpu.SemaphoreType.DMA((n_band,)),
             pltpu.SemaphoreType.DMA((ITERS, dirs, n_band - 1)),
@@ -549,15 +607,17 @@
     )(
         vis.reshape((2,) + half),
         coh.reshape(dirs, 8, times, base),
-        pack(jones_start),
-        pack(dual_start),
-        pack(cons0),
-        jnp.broadcast_to(row[:, None], (terms, LANES)),
-        ids.reshape(1, -1),
-        jnp.broadcast_to(ids[:, None], (2 * base, LANES)),
+        enter(jones_start.reshape((dirs, 4, 2, stations))),
+        enter(dual_start.reshape((dirs, 4, 2, stations))),
+        enter(consensus_start.reshape((terms, dirs, 4, 2, stations))),
+        freq_basis,
+        pairs,
     )
-    coeffs = coeffs.reshape(consensus_start.shape)
-    return unpack(jones), unpack(dual), coeffs
+    return (
+        leave(jones, jones_start.shape),
+        leave(dual, jones_start.shape),
+        leave(coeffs, consensus_start.shape),
+    )
 
 
 def solution(mesh):

time: 102 us -> 69.3 us (0.68)
  Pallas kernels: 86.6 us -> 63.9 us
  local copies, waits for them, and re-layouts: 14.1 us -> 4.57 us
    pallas_call x1, Pallas kernels: 86.6 us -> 63.9 us  [local(): pl.pallas_call(functools.partial(kernel, n_band, n_dir, dirs, times, base...]
    reshape x11 -> x0, local copies, waits for them, and re-layouts: 9.09 us -> none  [the longest x6 4.11 us: pack(): value = value.reshape(dirs, 8, per, LANES)]
    broadcast_in_dim x2 -> x0, local copies, waits for them, and re-layouts: 2.4 us -> none  [the longest x1 1.41 us: local(): jnp.broadcast_to(row[:, None], (terms, LANES))]
    unnamed x8 -> x5, local copies, waits for them, and re-layouts: 2.63 us -> 4.57 us
where the time goes in v2:
time: 69.3 us; the launch traced here: 69.1 us
  Pallas kernels  63.9 us (92%)
  local copies, waits for them, and re-layouts  4.57 us (7%)
    pallas_call x1, Pallas kernels, local(): pl.pallas_call(functools.partial(kernel, n_band, n_dir, dirs, times, base...  63.9 us
    unnamed x5, local copies, waits for them, and re-layouts  4.57 us

profile of v2, /device:TPU:0, one launch (start us, length us, event | category | flops | bytes accessed | tf_op | source)
XLA Modules:
  0.0 69.1 jit_solution(13947728614101849884)
XLA Ops:
  0.6 63.9 %shard_map.94 = (f32[4,4,16,128]{3,2,1,0:T(8,128)}, f32[4,4,16,128]{3,2,1,0:T(8,128)}, f32[8,4,4,16,128]{4,3,2,1,0:T(8,128)}) custom-call(f32[2,4,16,512]{3,2,1,0:T(8,128)} %bitcast.35, f32[4,8,16,512]{3,2,1,0:T(8,128)} %bitcast.32, f32[4,4,16,128]{3,2,1,0:T(8,128)} %bitcast.36, f32[4,4,16,128]{3,2,1,0:T(8,128)} %bitcast.37, f32[8,4,4,16,128]{4,3,2,1,0:T(8,128)} %bitcast.33, ...), custom_call_target="tpu_custom_call" | custom-call | tf_op jit(solution)/shard_map/pallas_call | solution.py:560
  64.6 0.0 copy-start
  64.6 1.6 %copy.19 = f32[1,4,2,2,2,1024]{5,4,3,2,1,0:T(2,128)} copy(f32[1,4,2,2,2,1024]{5,4,3,2,1,0:T(2,128)} %bitcast.39) | data formatting | bytes 262144
  66.2 0.0 copy-done
  66.2 0.7 copy.20
  66.8 2.3 %copy.21 = f32[8,4,2,2,2,1024]{5,4,3,2,1,0:T(2,128)} copy(f32[8,4,2,2,2,1024]{5,4,3,2,1,0:T(2,128)} %bitcast.34) | data formatting | bytes 2097152
Async XLA Ops:
  64.6 1.6 %copy-start = (f32[4,4,16,128]{3,2,1,0:T(8,128)S(1)}, f32[4,4,16,128]{3,2,1,0:T(8,128)}, u32[]{:S(2)}) copy-start(f32[4,4,16,128]{3,2,1,0:T(8,128)} %get-tuple-element.7) | copy-start | bytes 393220

commit v3 on v2

--- a/solution.py
+++ b/solution.py
@@ -238,7 +238,12 @@
     behind = n_band - 1 - ahead
 
     def slot_of(way, distance):
-        return distance if way == 0 or distance == 0 else ahead + distance
+        if distance > behind:
+            return n_band - 1
+        return distance + way * behind if distance else 0
+
+    def reach_of(k, way):
+        return ahead if way == k % 2 else behind
 
     def send_x(turn, k, way, distance):
         to = slot_of(way, distance + 1)
@@ -253,22 +258,24 @@
         copy.start()
         x_copies[turn][(k, way, distance + 1)] = copy
 
-    def pump(turn, distance):
-        for k in range(dirs):
-            for way, reach in enumerate((ahead, behind)):
+    def pump(turn, distance, chosen=range(dirs)):
+        for k in chosen:
+            for way in range(2):
+                reach = reach_of(k, way)
                 if distance <= reach:
                     x_copies[turn][(k, way, distance)].wait_recv()
                     if distance < reach:
                         send_x(turn, k, way, distance)
 
     def source(slot):
-        if slot <= ahead:
+        if slot <= behind:
             return at(lax.rem(pos + n_band - slot, n_band))
-        return at(lax.rem(pos + slot - ahead, n_band))
+        return at(lax.rem(pos + slot - behind, n_band))
 
     def end(comp, lane):
         return ends[comp * dirs : (comp + 1) * dirs, lane]
 
+    early, late = range(dirs // 2), range(dirs // 2, dirs)
     d_copies = []
 
     def send_d(turn, n, src, dst, stage):
@@ -338,7 +345,7 @@
         other = 1 - own
         hop = send_d(turn, 0, model.at[turn, other], got_a.at[turn], 0)
         if turn > 0:
-            pump(turn - 1, 1)
+            pump(turn - 1, 1, early)
 
         jp = [(end(v, first), end(4 + v, first)) for v in range(4)]
         jq = [(end(v, second), end(4 + v, second)) for v in range(4)]
@@ -374,6 +381,8 @@
         for stage in range(1, stages):
             hop = send_d(turn, stage, sum_a.at[turn, stage - 1], got_b.at[turn, stage - 1], stage)
             if stage == 1:
+                if turn > 0:
+                    pump(turn - 1, 1, late)
                 split_store(lhs_n, 4 * dirs, vals_n[...])
                 found = join(jnp.dot(lhs_n[...], scatter_hot[...], preferred_element_type=f32), 4 * dirs)
                 for g in range(4 * dirs // SUB):
@@ -393,10 +402,12 @@
         hop = send_d(turn, stages, sum_b.at[turn], got_c.at[turn], 0)
         if turn > 0:
             for s in range(max(2, (ahead + 2) // 2), ahead):
-                pump(turn - 1, s)
+                pump(turn - 1, s, early if s + 1 == ahead else range(dirs))
         res[own] = vis[own] - sum_b[turn]
         hop.wait_recv()
         res[other] = vis[other] - got_c[turn]
+        if turn > 0 and ahead - 1 >= max(2, (ahead + 2) // 2):
+            pump(turn - 1, ahead - 1, late)
 
         def cross_body(j, carry):
             lane = pl.ds(pl.multiple_of(j * LANES, LANES), LANES)
@@ -503,8 +514,8 @@
                         if turn + 1 == ITERS:
                             jones_out[halves_of(k, v)] = value
                         xall[turn, k, 0, v] = value + dual[here, :] * (1.0 / RHO)
-            for way, reach in enumerate((ahead, behind)):
-                if reach:
+            for way in range(2):
+                if reach_of(k, way):
                     send_x(turn, k, way, 0)
 
     last = ITERS - 1

time: 69.3 us -> 69.1 us (level)
  no operation moved by 1% of the time
where the time goes in v3:
time: 69.1 us; the launch traced here: 68.9 us
  Pallas kernels  63.7 us (92%)
  local copies, waits for them, and re-layouts  4.57 us (7%)
    pallas_call x1, Pallas kernels, local(): pl.pallas_call(functools.partial(kernel, n_band, n_dir, dirs, times, base...  63.7 us
    unnamed x5, local copies, waits for them, and re-layouts  4.57 us

profile of v3, /device:TPU:0, one launch (start us, length us, event | category | flops | bytes accessed | tf_op | source)
XLA Modules:
  0.0 68.9 jit_solution(13848063762511590861)
XLA Ops:
  0.6 63.7 %shard_map.94 = (f32[4,4,16,128]{3,2,1,0:T(8,128)}, f32[4,4,16,128]{3,2,1,0:T(8,128)}, f32[8,4,4,16,128]{4,3,2,1,0:T(8,128)}) custom-call(f32[2,4,16,512]{3,2,1,0:T(8,128)} %bitcast.35, f32[4,8,16,512]{3,2,1,0:T(8,128)} %bitcast.32, f32[4,4,16,128]{3,2,1,0:T(8,128)} %bitcast.36, f32[4,4,16,128]{3,2,1,0:T(8,128)} %bitcast.37, f32[8,4,4,16,128]{4,3,2,1,0:T(8,128)} %bitcast.33, ...), custom_call_target="tpu_custom_call" | custom-call | tf_op jit(solution)/shard_map/pallas_call | solution.py:571
  64.3 0.0 copy-start
  64.3 1.6 %copy.19 = f32[1,4,2,2,2,1024]{5,4,3,2,1,0:T(2,128)} copy(f32[1,4,2,2,2,1024]{5,4,3,2,1,0:T(2,128)} %bitcast.39) | data formatting | bytes 262144
  66.0 0.0 copy-done
  66.0 0.7 copy.20
  66.6 2.3 %copy.21 = f32[8,4,2,2,2,1024]{5,4,3,2,1,0:T(2,128)} copy(f32[8,4,2,2,2,1024]{5,4,3,2,1,0:T(2,128)} %bitcast.34) | data formatting | bytes 2097152
Async XLA Ops:
  64.3 1.6 %copy-start = (f32[4,4,16,128]{3,2,1,0:T(8,128)S(1)}, f32[4,4,16,128]{3,2,1,0:T(8,128)}, u32[]{:S(2)}) copy-start(f32[4,4,16,128]{3,2,1,0:T(8,128)} %get-tuple-element.7) | copy-start | bytes 393220

commit v4 on v3

--- a/solution.py
+++ b/solution.py
@@ -344,9 +344,6 @@
 
         other = 1 - own
         hop = send_d(turn, 0, model.at[turn, other], got_a.at[turn], 0)
-        if turn > 0:
-            pump(turn - 1, 1, early)
-
         jp = [(end(v, first), end(4 + v, first)) for v in range(4)]
         jq = [(end(v, second), end(4 + v, second)) for v in range(4)]
 
@@ -376,6 +373,8 @@
             vals_n[n * dirs : (n + 1) * dirs, first] = left
             vals_n[n * dirs : (n + 1) * dirs, second] = right
 
+        if turn > 0:
+            pump(turn - 1, 1, early)
         hop.wait_recv()
         sum_a[turn, 0] = model[turn, own] + got_a[turn]
         for stage in range(1, stages):

time: 69.1 us -> 69.1 us (level)
  no operation moved by 1% of the time
where the time goes in v4:
time: 69.1 us; the launch traced here: 68.9 us
  Pallas kernels  63.7 us (92%)
  local copies, waits for them, and re-layouts  4.57 us (7%)
    pallas_call x1, Pallas kernels, local(): pl.pallas_call(functools.partial(kernel, n_band, n_dir, dirs, times, base...  63.7 us
    unnamed x5, local copies, waits for them, and re-layouts  4.57 us

profile of v4, /device:TPU:0, one launch (start us, length us, event | category | flops | bytes accessed | tf_op | source)
XLA Modules:
  0.0 68.9 jit_solution(2636064341035616390)
XLA Ops:
  0.6 63.7 %shard_map.94 = (f32[4,4,16,128]{3,2,1,0:T(8,128)}, f32[4,4,16,128]{3,2,1,0:T(8,128)}, f32[8,4,4,16,128]{4,3,2,1,0:T(8,128)}) custom-call(f32[2,4,16,512]{3,2,1,0:T(8,128)} %bitcast.35, f32[4,8,16,512]{3,2,1,0:T(8,128)} %bitcast.32, f32[4,4,16,128]{3,2,1,0:T(8,128)} %bitcast.36, f32[4,4,16,128]{3,2,1,0:T(8,128)} %bitcast.37, f32[8,4,4,16,128]{4,3,2,1,0:T(8,128)} %bitcast.33, ...), custom_call_target="tpu_custom_call" | custom-call | tf_op jit(solution)/shard_map/pallas_call | solution.py:570
  64.3 0.0 copy-start
  64.3 1.6 %copy.19 = f32[1,4,2,2,2,1024]{5,4,3,2,1,0:T(2,128)} copy(f32[1,4,2,2,2,1024]{5,4,3,2,1,0:T(2,128)} %bitcast.39) | data formatting | bytes 262144
  66.0 0.0 copy-done
  66.0 0.7 copy.20
  66.6 2.3 %copy.21 = f32[8,4,2,2,2,1024]{5,4,3,2,1,0:T(2,128)} copy(f32[8,4,2,2,2,1024]{5,4,3,2,1,0:T(2,128)} %bitcast.34) | data formatting | bytes 2097152
Async XLA Ops:
  64.3 1.6 %copy-start = (f32[4,4,16,128]{3,2,1,0:T(8,128)S(1)}, f32[4,4,16,128]{3,2,1,0:T(8,128)}, u32[]{:S(2)}) copy-start(f32[4,4,16,128]{3,2,1,0:T(8,128)} %get-tuple-element.7) | copy-start | bytes 393220
